TPU v7x, 256 devices: a whole 4x4x8 slice. The times are simulated.
256 devices in a mesh: gz: 64 (over y, z, core), ga: 4 (over x).
Axes of the slice: x: 4, y: 4, z: 8, core: 2. Of those that a mesh axis runs over, the one named last changes fastest.
Arguments:
- solution: float32 [512, 256, 256], P(('gz', 'ga')), may hold values from -6 to 6
- residual: float32 [512, 256, 256], P(('gz', 'ga')), may hold values from -40 to 40
- direction: float32 [512, 256, 256], P(('gz', 'ga')), may hold values from -40 to 40
Outputs:
- solution_out: float32 [512, 256, 256], P(('gz', 'ga'))
- residual_out: float32 [512, 256, 256], P(('gz', 'ga'))
- direction_out: float32 [512, 256, 256], P(('gz', 'ga'))
All inputs are finite; a program needn't handle non-finite values.
Results may differ from a plain program's by a relative error of at most 0.0003.
Values sent between devices are 32-bit elements; how exact they have to be, the bound alone decides.
No kernel may reach another device: no remote copies, remote signals or barrier semaphores. Data moves between devices by JAX's collectives and lax.ppermute only.
A program may use at most 128 MiB of HBM per device.

v0:
```python
import functools

import jax
import jax.numpy as jnp
import numpy as np
from jax import lax
from jax.experimental import pallas as pl
from jax.experimental.pallas import tpu as pltpu
from jax.sharding import Mesh, PartitionSpec as P

S = 8
COLS = 2 * S + 1
PLANES = 8
HALO = 8
LANES = 256
TALL = PLANES + 2 * HALO
FIRST = -1.0 / 6.0
NEXT = -1.0 / 3.0
ALL = ("zz", "c", "x")

DD, RR, DR = 0, 2 * S + 1, 4 * S
SUMS = 6 * S


def chain_kernel(place, own, side, across, basis, sums, ext_d, ext_r, parts):
    rows = own.shape[3]
    keep = rows - 2 * HALO
    core, first, last, low_x, high_x = (place[i] for i in range(5))

    row = lax.broadcasted_iota(jnp.int32, (rows, LANES), 0)
    lane = lax.broadcasted_iota(jnp.int32, (rows, LANES), 1)
    inside = jnp.logical_and(
        jnp.logical_or(row >= HALO, low_x == 0), jnp.logical_or(row < rows - HALO, high_x == 0)
    ).astype(jnp.float32)
    left_edge, right_edge = lane == 0, lane == LANES - 1

    def fold(product):
        total = jnp.sum(product.reshape(keep // 8, 8, LANES), axis=0)
        return total[:, :128] + total[:, 128:]

    for field, ext in ((0, ext_d), (1, ext_r)):
        for plane in range(PLANES):
            ext[0, HALO + plane] = own[plane // 2, field, plane % 2]

        @pl.when(core == 0)
        def _():
            for plane in range(PLANES):
                ext[0, plane] = across[plane // 2, field, plane % 2]
                ext[0, HALO + PLANES + plane] = side[plane // 2, field, plane % 2]

        @pl.when(core != 0)
        def _():
            for plane in range(PLANES):
                ext[0, plane] = side[plane // 2, field, plane % 2]
                ext[0, HALO + PLANES + plane] = across[plane // 2, field, plane % 2]

    def stencil(ext, now, plane):
        here = ext[now, plane]
        total = ext[now, plane - 1] + ext[now, plane + 1]
        total = total + pltpu.roll(here, 1, 0) + pltpu.roll(here, rows - 1, 0)
        left = jnp.where(left_edge, 0.0, pltpu.roll(here, 1, 1))
        right = jnp.where(right_edge, 0.0, pltpu.roll(here, LANES - 1, 1))
        return here, total + (left + right)

    def advance(ext, power, column, visit):
        now, new = (power - 1) % 3, power % 3
        old = (power - 2) % 3
        scale = FIRST if power == 1 else NEXT

        def one(plane, factor):
            here, total = stencil(ext, now, plane)
            value = total * factor
            if power > 1:
                value = value - ext[old, plane]
            ext[new, plane] = value
            return here, value

        def outer(factor):
            def body(plane, _):
                one(plane, factor)
                return 0

            return body

        lax.fori_loop(power, HALO, outer(inside * (scale * first)), 0)

        def body(plane, accs):
            here, value = one(HALO + plane, inside * scale)
            here, value = here[HALO : HALO + keep], value[HALO : HALO + keep]
            basis[column, plane] = value
            return visit(accs, plane, here, value)

        accs = lax.fori_loop(0, PLANES, body, tuple(jnp.zeros((8, 128), jnp.float32) for _ in range(visit.count)))
        lax.fori_loop(HALO + PLANES, TALL - power, outer(inside * (scale * last)), 0)
        return accs

    def of_own(accs, plane, here, value):
        return accs[0] + fold(value * value), accs[1] + fold(here * value)

    of_own.count = 2

    def put(index, acc):
        parts[pl.ds(index, 1), :] = jnp.sum(acc, axis=0, keepdims=True)

    parts[...] = jnp.zeros_like(parts)

    def start(plane, accs):
        d = ext_d[0, HALO + plane, HALO : HALO + keep]
        r = ext_r[0, HALO + plane, HALO : HALO + keep]
        basis[0, plane] = d
        basis[S + 1, plane] = r
        return accs[0] + fold(d * d), accs[1] + fold(r * r), accs[2] + fold(d * r)

    zero = jnp.zeros((8, 128), jnp.float32)
    dd, rr, dr = lax.fori_loop(0, PLANES, start, (zero, zero, zero))
    put(DD, dd)
    put(RR, rr)
    put(DR, dr)

    for power in range(1, S + 1):
        same, next_to = advance(ext_d, power, power, of_own)
        put(DD + 2 * power, same)
        put(DD + 2 * power - 1, next_to)

    def ahead(plane, acc):
        return acc + fold(basis[1, plane] * basis[S + 1, plane])

    put(DR + 1, lax.fori_loop(0, PLANES, ahead, zero))

    for power in range(1, S):

        def visit(accs, plane, here, value, power=power):
            return (
                accs[0] + fold(value * value),
                accs[1] + fold(here * value),
                accs[2] + fold(basis[power, plane] * value),
                accs[3] + fold(basis[power + 1, plane] * value),
            )

        visit.count = 4
        same, next_to, cross, cross_next = advance(ext_r, power, S + 1 + power, visit)
        put(RR + 2 * power, same)
        put(RR + 2 * power - 1, next_to)
        put(DR + 2 * power, cross)
        put(DR + 2 * power + 1, cross_next)

    sums[...] = jnp.sum(parts[...].T, axis=0, keepdims=True)


def coefficients(sums):
    tall = 24
    shape = (tall, 128)
    i = lax.broadcasted_iota(jnp.int32, shape, 0)
    j = lax.broadcasted_iota(jnp.int32, shape, 1)
    row_r, col_r = i > S, j > S
    a = jnp.where(row_r, i - (S + 1), i)
    b = jnp.where(col_r, j - (S + 1), j)
    valid = jnp.logical_and(i < COLS, j < COLS)
    base = jnp.where(row_r, jnp.where(col_r, RR, DR), jnp.where(col_r, DR, DD))
    plus = a + b
    minus = jnp.abs(a - b)
    odd = plus & 1
    at_plus = jnp.where(valid, base + plus, -1)
    at_minus = jnp.where(valid, base + minus, -1)
    at_base = jnp.where(valid, base + odd, -1)
    gram = jnp.zeros(shape, jnp.float32)
    for place in range(SUMS):
        weight = (
            (at_plus == place).astype(jnp.float32)
            + (at_minus == place).astype(jnp.float32)
            - (at_base == place).astype(jnp.float32)
        )
        gram = gram + weight * sums[:, place : place + 1]

    def change(index, axis):
        second = index > S
        k = jnp.where(second, index - (S + 1), index)
        count = jnp.where(second, S, S + 1)
        valid = index < COLS
        middle = jnp.where(jnp.logical_and(valid, k < count - 1), 6.0, 0.0)
        below = jnp.where(jnp.logical_and(valid, k >= 1), jnp.where(k == 1, 6.0, 3.0), 0.0)
        above = jnp.where(jnp.logical_and(valid, k + 1 < count - 1), 3.0, 0.0)
        size = shape[axis]

        def apply(v):
            return middle * v + below * pltpu.roll(v, 1, axis) + above * pltpu.roll(v, size - 1, axis)

        return apply

    down, along = change(i, 0), change(j, 1)

    def quadratic(left_down, right_along):
        return jnp.sum(left_down * (gram * right_along), keepdims=True)

    def unit(index, k):
        return (index == k).astype(jnp.float32)

    q_d, q_a = unit(i, 0), unit(j, 0)
    w_d, w_a = unit(i, S + 1), unit(j, S + 1)
    c_d = jnp.zeros(shape, jnp.float32)
    rho = quadratic(w_d, w_a)
    for _ in range(S):
        m_d, m_a = down(q_d), along(q_a)
        alpha = rho / quadratic(q_d, m_a)
        c_d = c_d + alpha * q_d
        w_d, w_a = w_d - alpha * m_d, w_a - alpha * m_a
        rho_new = quadratic(w_d, w_a)
        beta = rho_new / rho
        q_d, q_a = w_d + beta * q_d, w_a + beta * q_a
        rho = rho_new
    return c_d, w_d, q_d


def combine_kernel(sums, basis, out, coefs):
    total = jnp.sum(sums[...], axis=0, keepdims=True)
    for which, value in enumerate(coefficients(total)):
        coefs[which] = value
    keep = basis.shape[2]
    tile = 16
    splat = {}

    def body(step, _):
        plane = step // (keep // tile)
        row = pl.multiple_of((step % (keep // tile)) * tile, tile)
        accs = [None] * 3
        for k in range(COLS):
            v = basis[k, plane, pl.ds(row, tile)]
            for which in range(3):
                factor = coefs[which, k : k + 1, :]
                term = v * jnp.concatenate([factor, factor], axis=1)
                accs[which] = term if accs[which] is None else accs[which] + term
        for which in range(3):
            out[plane // 2, which, plane % 2, pl.ds(row, tile)] = accs[which]
        return 0

    lax.fori_loop(0, PLANES * (keep // tile), body, 0)


def on_device(solution, residual, direction):
    groups = lax.axis_size("x")
    x, c, zz = lax.axis_index("x"), lax.axis_index("c"), lax.axis_index("zz")
    outer = lax.axis_size("zz")
    per, height, lanes = direction.shape
    keep = height // groups
    rows = keep + 2 * HALO

    fields = jnp.pad(jnp.stack([direction, residual]), ((0, 0), (0, 0), (HALO, HALO), (0, 0)))
    pieces = jnp.stack([fields[:, :, g * keep : g * keep + rows] for g in range(groups)])
    own = lax.all_to_all(pieces, "x", 0, 0, tiled=True)

    blocks = 2 * outer
    near = [(b, b - 1) for b in range(0, blocks, 2) if b > 0] + [(b, b + 1) for b in range(1, blocks, 2) if b + 1 < blocks]
    across = lax.ppermute(own, ("zz", "c"), near)
    side = lax.ppermute(own, "c", [(0, 1), (1, 0)])

    place = jnp.stack(
        [
            c,
            1 - jnp.logical_and(zz == 0, c == 0).astype(jnp.int32),
            1 - jnp.logical_and(zz == outer - 1, c == 1).astype(jnp.int32),
            (x == 0).astype(jnp.int32),
            (x == groups - 1).astype(jnp.int32),
        ]
    ).astype(jnp.int32)

    vmem = pl.BlockSpec(memory_space=pltpu.VMEM)
    basis, sums = pl.pallas_call(
        chain_kernel,
        out_shape=(
            jax.ShapeDtypeStruct((COLS, PLANES, keep, lanes), jnp.float32),
            jax.ShapeDtypeStruct((1, 128), jnp.float32),
        ),
        in_specs=[pl.BlockSpec(memory_space=pltpu.SMEM), vmem, vmem, vmem],
        out_specs=(vmem, vmem),
        scratch_shapes=[
            pltpu.VMEM((3, TALL, rows, lanes), jnp.float32),
            pltpu.VMEM((3, TALL, rows, lanes), jnp.float32),
            pltpu.VMEM((128, 128), jnp.float32),
        ],
        compiler_params=pltpu.CompilerParams(vmem_limit_bytes=40 * 2**20),
        name="chains",
    )(place, own, side, across)

    devices = groups * blocks
    everyone = lax.all_to_all(jnp.broadcast_to(sums[None], (devices, 1, 128)), ALL, 0, 0, tiled=True)

    mixed = pl.pallas_call(
        combine_kernel,
        out_shape=jax.ShapeDtypeStruct((groups, 3, per, keep, lanes), jnp.float32),
        in_specs=[vmem, vmem],
        out_specs=vmem,
        scratch_shapes=[pltpu.VMEM((3, 24, 128), jnp.float32)],
        compiler_params=pltpu.CompilerParams(vmem_limit_bytes=20 * 2**20),
        name="combine",
    )(everyone.reshape(devices, 128), basis)

    back = lax.all_to_all(mixed, "x", 0, 0, tiled=True)
    whole = [jnp.swapaxes(back[:, which], 0, 1).reshape(per, height, lanes) for which in range(3)]
    return solution + whole[0], whole[1], whole[2]


def solution(mesh):
    blocks, groups = mesh.devices.shape
    split = Mesh(mesh.devices.reshape(blocks // 2, 2, groups), ALL)
    spec = P(ALL, None, None)
    return jax.shard_map(
        on_device, mesh=split, in_specs=(spec, spec, spec), out_specs=(spec, spec, spec), check_vma=False
    )
```

profile of v0, /device:TPU:1, one launch (start us, length us, event | category | flops | bytes accessed | tf_op | source)
XLA Modules:
  0.0 130.7 jit_solution(3497621646358924959)
XLA Ops:
  0.6 0.0 copy-start.1
  0.6 0.0 copy-start
  0.7 1.4 %pad_maximum_fusion = f32[2,2,256,256]{3,2,1,0:T(8,128)S(1)} fusion(f32[1,2,256,256]{3,2,1,0:T(8,128)} %bitcast.35, f32[1,2,256,256]{3,2,1,0:T(8,128)} %bitcast.37), kind=kLoop, calls=%fused_computation.2 | loop fusion | flops 262144 | bytes 2097152 | tf_op jit(solution)/shard_map/stack | solution.py:247
  2.0 0.0 copy-done.1
  2.0 0.1 copy-done
  2.1 0.1 fusion
  2.3 0.1 pad_maximum_fusion.1
  2.4 21.6 %all_to_all.15.own = f32[4,2,2,80,256]{4,3,2,1,0:T(8,128)S(1)} all-to-all(f32[4,2,2,80,256]{4,3,2,1,0:T(8,128)S(1)} %pad_maximum_fusion.1), channel_id=1, replica_groups=mesh['zz'=32,'c'=2,'x'=4] {'x'}, dimensions={0} | all-to-all | bytes 2621440 | tf_op jit(solution)/shard_map/all_to_all | solution.py:249
  24.0 5.3 %collective-permute-start.1 = (f32[4,2,2,80,256]{4,3,2,1,0:T(8,128)S(1)}, f32[4,2,2,80,256]{4,3,2,1,0:T(8,128)S(1)}, u32[]{:S(2)}, u32[]{:S(2)}) collective-permute-start(f32[4,2,2,80,256]{4,3,2,1,0:T(8,128)S(1)} %all_to_all.15.own), channel_id=1, source_target_pairs={{8,4},{16,12},{24,20},{32,28},{40,36},{48,44},{56,52},{64,60},{72,... | collective-permute-start | bytes 3932168 | tf_op jit(solution)/shard_map/ppermute | solution.py:253
  29.3 0.1 collective-permute-start
  29.4 0.1 stack.55.place
  29.5 15.1 %collective-permute-done.1.across = f32[4,2,2,80,256]{4,3,2,1,0:T(8,128)S(1)} collective-permute-done((f32[4,2,2,80,256]{4,3,2,1,0:T(8,128)S(1)}, f32[4,2,2,80,256]{4,3,2,1,0:T(8,128)S(1)}, u32[]{:S(2)}, u32[]{:S(2)}) %collective-permute-start.1) | collective-permute-done | bytes 1310752 | tf_op jit(solution)/shard_map/ppermute | solution.py:253
  44.6 0.0 collective-permute-done.side
  44.6 29.2 %chains.1 = (f32[17,8,64,256]{3,2,1,0:T(8,128)S(1)}, f32[1,128]{1,0:T(1,128)S(1)}) custom-call(s32[5]{0:T(128)S(1)} %stack.55.place, f32[4,2,2,80,256]{4,3,2,1,0:T(8,128)S(1)} %all_to_all.15.own, f32[4,2,2,80,256]{4,3,2,1,0:T(8,128)} %collective-permute-done.side, f32[4,2,2,80,256]{4,3,2,1,0:T(8,128)S(1)} %collective-permute-done.1.across), custom_call_target="tpu_custom_call" | custom-call | tf_op jit(solution)/shard_map/chains/pallas_call | solution.py:267
  73.8 0.1 broadcast_in_dim.9
  73.9 26.3 %all_to_all.16 = f32[256,1,128]{2,1,0:T(1,128)S(1)} all-to-all(f32[256,1,128]{2,1,0:T(1,128)S(1)} %broadcast_in_dim.9), channel_id=1, replica_groups=mesh['zz'=32,'c'=2,'x'=4] {'zz','c','x'}, dimensions={0} | all-to-all | bytes 262144 | tf_op jit(solution)/shard_map/all_to_all | solution.py:285
  100.2 5.2 %combine.1 = f32[4,3,2,64,256]{4,3,2,1,0:T(8,128)S(1)} custom-call(f32[256,128]{1,0:T(8,128)S(1)} %bitcast.33, f32[17,8,64,256]{3,2,1,0:T(8,128)S(1)} %get-tuple-element.6.basis), custom_call_target="tpu_custom_call" | custom-call | tf_op jit(solution)/shard_map/combine/pallas_call | solution.py:287
  105.4 22.3 %all_to_all.17 = f32[4,3,2,64,256]{4,3,2,1,0:T(8,128)S(1)} all-to-all(f32[4,3,2,64,256]{4,3,2,1,0:T(8,128)S(1)} %combine.1), channel_id=1, replica_groups=mesh['zz'=32,'c'=2,'x'=4] {'x'}, dimensions={0} | all-to-all | bytes 3145728 | tf_op jit(solution)/shard_map/all_to_all | solution.py:297
  127.7 0.1 slice_bitcast_fusion
  127.8 0.8 copy.11
  128.7 0.0 copy-start.2
  128.7 0.8 copy.10
  129.5 0.3 copy-done.2
  129.9 0.9 bitcast_add_fusion
  (1 shorter events, 0.0 us)
Async XLA Ops:
  0.6 1.4 %copy-start.1 = (f32[2,256,256]{2,1,0:T(8,128)S(1)}, f32[2,256,256]{2,1,0:T(8,128)}, u32[]{:S(2)}) copy-start(f32[2,256,256]{2,1,0:T(8,128)} %param.5) | copy-start | bytes 1572868
  0.6 1.5 %copy-start = (f32[2,256,256]{2,1,0:T(8,128)S(1)}, f32[2,256,256]{2,1,0:T(8,128)}, u32[]{:S(2)}) copy-start(f32[2,256,256]{2,1,0:T(8,128)} %param.4) | copy-start | bytes 1572868
  24.0 20.6 %collective-permute-start.1 = (f32[4,2,2,80,256]{4,3,2,1,0:T(8,128)S(1)}, f32[4,2,2,80,256]{4,3,2,1,0:T(8,128)S(1)}, u32[]{:S(2)}, u32[]{:S(2)}) collective-permute-start(f32[4,2,2,80,256]{4,3,2,1,0:T(8,128)S(1)} %all_to_all.15.own), channel_id=1, source_target_pairs={{8,4},{16,12},{24,20},{32,28},{40,36},{48,44},{56,52},{64,60},{72,... | collective-permute-start | bytes 3932168 | tf_op jit(solution)/shard_map/ppermute | solution.py:253
  29.3 15.3 %collective-permute-start = (f32[4,2,2,80,256]{4,3,2,1,0:T(8,128)S(1)}, f32[4,2,2,80,256]{4,3,2,1,0:T(8,128)}, u32[]{:S(2)}, u32[]{:S(2)}) collective-permute-start(f32[4,2,2,80,256]{4,3,2,1,0:T(8,128)S(1)} %all_to_all.15.own), channel_id=1, source_target_pairs={{0,4},{4,0},{1,5},{5,1},{2,6},{6,2},{3,7},{7,3},{8,12},{12,8},{9,1... | collective-permute-start | bytes 3932168 | tf_op jit(solution)/shard_map/ppermute | solution.py:254
  128.7 1.2 copy-start.2
where the time goes:
time: 131 us
  blocking collectives  70.2 us (54%)
  Pallas kernels  34.4 us (26%)
  waiting for transfers between devices  15.1 us (12%)
  starting transfers between devices  5.37 us (4%)
  local copies, waits for them, and re-layouts  2.5 us (2%)
  other arithmetic  2.46 us (2%)
    pallas_call x1, Pallas kernels, on_device(): pl.pallas_call(chain_kernel, out_shape=(jax.ShapeDtypeStruct((COLS, PLANE...  29.2 us
    all_to_all x1, blocking collectives, on_device(): lax.all_to_all(jnp.broadcast_to(sums[None], (devices, 1, 128)), ALL, 0, 0...  26.3 us
    all_to_all x1, blocking collectives, on_device(): back = lax.all_to_all(mixed, 'x', 0, 0, tiled=True)  22.3 us
    all_to_all x1, blocking collectives, on_device(): own = lax.all_to_all(pieces, 'x', 0, 0, tiled=True)  21.6 us
    ppermute x1, waiting for transfers between devices, on_device(): across = lax.ppermute(own, ('zz', 'c'), near)  15.1 us
    ppermute x1, starting transfers between devices, on_device(): across = lax.ppermute(own, ('zz', 'c'), near)  5.28 us
    pallas_call x1, Pallas kernels, on_device(): pl.pallas_call(combine_kernel, out_shape=jax.ShapeDtypeStruct((groups, 3,...  5.2 us
  transfers between devices with their start and end apart: 2, of which 1 were waited for; matrix products, arithmetic and copies ran while one was open for 0% of the time, Pallas kernels for 0%

commit v1 on v0

v1 whole, which is shorter than its diff:
```python
import functools

import jax
import jax.numpy as jnp
import numpy as np
from jax import lax
from jax.experimental import pallas as pl
from jax.experimental.pallas import tpu as pltpu
from jax.sharding import Mesh, PartitionSpec as P

S = 8
COLS = 2 * S + 1
PLANES = 8
HALO = 8
PAD = 8
HALF = 128
GROUP = 4
FIRST = -1.0 / 6.0
NEXT = -1.0 / 3.0
ALL = ("zz", "c", "x")
VMEM = pl.BlockSpec(memory_space=pltpu.VMEM)
SMEM = pl.BlockSpec(memory_space=pltpu.SMEM)
HBM = pl.BlockSpec(memory_space=pltpu.HBM)

DD, RR, DR = 0, 2 * S + 1, 4 * S
SUMS = 6 * S


def chain_plan(steps):
    lows = [HALO - steps + k for k in range(steps + 1)]
    groups = [0] + [-(-(PLANES + 2 * (steps - k)) // GROUP) for k in range(1, steps + 1)]
    held = []
    for k in range(steps + 1):
        own = GROUP * groups[k] if k else PLANES + 2 * steps
        read = GROUP * groups[k + 1] + 2 if k < steps else 0
        held.append(max(own, read))
    return lows, groups, held


def pack_kernel(direction, residual, out_d, out_r, sem):
    pieces, per, halves, rows, _ = out_d.shape
    height = direction.shape[1]
    keep = rows - 2 * HALO
    copies = []
    for source, out in ((direction, out_d), (residual, out_r)):
        for g in range(pieces):
            low = max(g * keep - HALO, 0)
            high = min((g + 1) * keep + HALO, height)
            at = low - (g * keep - HALO)
            for h in range(halves):
                copies.append(
                    pltpu.make_async_copy(
                        source.at[:, pl.ds(low, high - low), pl.ds(h * HALF, HALF)],
                        out.at[g, :, h, pl.ds(at, high - low), :],
                        sem.at[len(copies)],
                    )
                )
    for copy in copies:
        copy.start()
    for out in (out_d, out_r):
        zeros = jnp.zeros((per, halves, HALO, HALF), jnp.float32)
        out[0, :, :, :HALO] = zeros
        out[pieces - 1, :, :, rows - HALO :] = zeros
    for copy in copies:
        copy.wait()


def run_chain(place, own, side, across, chain, sideways, steps):
    lows, groups, _ = chain_plan(steps)
    rows = own.shape[3]
    core = place[0]
    data = pl.ds(PAD, rows)

    def load(target, source, plane):
        for h in range(2):
            chain[0][target - lows[0], h, data] = source[plane // 2, plane % 2, h]

    for plane in range(PLANES):
        load(HALO + plane, own, plane)

    def halo(low, high):
        for plane in range(PLANES - steps, PLANES):
            load(plane, low, plane)
        for plane in range(steps):
            load(HALO + PLANES + plane, high, plane)

    @pl.when(core == 0)
    def _():
        halo(across, side)

    @pl.when(core != 0)
    def _():
        halo(side, across)

    lane = lax.broadcasted_iota(jnp.int32, (rows, HALF), 1)
    at_low, at_high = lane == 0, lane == HALF - 1

    def neighbours_y(power, plane, u):
        source = chain[power - 1]
        index = plane + u - lows[power - 1]
        a, b = source[index, 0, data], source[index, 1, data]
        up_a, up_b = pltpu.roll(a, 1, 1), pltpu.roll(b, 1, 1)
        down_a, down_b = pltpu.roll(a, HALF - 1, 1), pltpu.roll(b, HALF - 1, 1)
        first = jnp.where(at_low, 0.0, up_a) + jnp.where(at_high, down_b, down_a)
        second = jnp.where(at_low, up_a, up_b) + jnp.where(at_high, 0.0, down_b)
        return first, second

    low_valid, high_valid, low_x, high_x = (place[i].astype(jnp.float32) for i in range(1, 5))

    def values(power, plane, u):
        now, new = chain[power - 1], chain[power]
        index = plane + u - lows[power - 1]
        where = plane + u
        scale = FIRST if power == 1 else NEXT
        outside_low = jnp.logical_and(where < HALO, place[1] == 0)
        outside_high = jnp.logical_and(where >= HALO + PLANES, place[2] == 0)
        scale = jnp.where(jnp.logical_or(outside_low, outside_high), 0.0, scale)
        for h in range(2):
            total = now[index - 1, h, data] + now[index + 1, h, data]
            total = total + (now[index, h, pl.ds(PAD - 1, rows)] + now[index, h, pl.ds(PAD + 1, rows)])
            total = total + sideways[u, h]
            parts = []
            for a, b, weight in ((0, HALO, low_x), (HALO, rows - HALO, None), (rows - HALO, rows, high_x)):
                factor = scale if weight is None else scale * weight
                parts.append(total[a:b] * factor)
            value = jnp.concatenate(parts, axis=0)
            if power > 1:
                value = value - chain[power - 2][plane + u - lows[power - 2], h, data]
            new[plane + u - lows[power], h, data] = value

    def group(power, plane, then):
        ahead = [neighbours_y(*then, u) for u in range(GROUP)] if then else []
        for u in range(GROUP):
            values(power, plane, u)
        for u, pair in enumerate(ahead):
            sideways[u, 0], sideways[u, 1] = pair

    for u in range(GROUP):
        sideways[u, 0], sideways[u, 1] = neighbours_y(1, lows[1], u)
    for power in range(1, steps + 1):

        def body(g, _, power=power):
            plane = lows[power] + GROUP * g
            group(power, plane, (power, plane + GROUP))
            return 0

        lax.fori_loop(0, groups[power] - 1, body, 0)
        last = lows[power] + GROUP * (groups[power] - 1)
        group(power, last, (power + 1, lows[power + 1]) if power < steps else None)


def own_of(chain, steps, k, plane, h, row):
    low = chain_plan(steps)[0][k]
    return chain[k][HALO + plane - low, h, pl.ds(row, 8)]


def products(count, keep, terms):
    def body(step, accs):
        plane, tile = step // (keep // 8), step % (keep // 8)
        row = pl.multiple_of(PAD + HALO + 8 * tile, 8)
        for h in range(2):
            accs = tuple(acc + x * y for acc, (x, y) in zip(accs, terms(plane, h, row)))
        return accs

    zero = jnp.zeros((8, HALF), jnp.float32)
    return lax.fori_loop(0, PLANES * (keep // 8), body, (zero,) * count)


def chain_terms(values):
    terms = [(values[0], values[0])]
    for k in range(1, len(values)):
        terms += [(values[k - 1], values[k]), (values[k], values[k])]
    return terms


def direction_kernel(place, own, side, across, *refs):
    chain, parts, sideways = refs[: S + 1], refs[S + 1], refs[S + 2]
    run_chain(place, own, side, across, chain, sideways, S)
    keep = own.shape[3] - 2 * HALO
    sums = products(
        2 * S + 1,
        keep,
        lambda plane, h, row: chain_terms([own_of(chain, S, k, plane, h, row) for k in range(S + 1)]),
    )
    parts[...] = jnp.zeros_like(parts)
    for k, total in enumerate(sums):
        parts[pl.ds(DD + k, 1), :] = jnp.sum(total, axis=0, keepdims=True)


def residual_kernel(place, own, side, across, *refs):
    other, parts_d, chain, sums, sideways, parts = (
        refs[: S + 1],
        refs[S + 1],
        refs[S + 2 : 2 * S + 2],
        refs[2 * S + 2],
        refs[2 * S + 3],
        refs[2 * S + 4],
    )
    run_chain(place, own, side, across, chain, sideways, S - 1)
    keep = own.shape[3] - 2 * HALO
    parts[...] = parts_d[...]

    def put(index, total):
        parts[pl.ds(index, 1), :] = jnp.sum(total, axis=0, keepdims=True)

    of_r = products(
        2 * S - 1,
        keep,
        lambda plane, h, row: chain_terms([own_of(chain, S - 1, k, plane, h, row) for k in range(S)]),
    )
    for k, total in enumerate(of_r):
        put(RR + k, total)

    def cross(plane, h, row):
        d = [own_of(other, S, k, plane, h, row) for k in range(S + 1)]
        r = [own_of(chain, S - 1, k, plane, h, row) for k in range(S)]
        terms = []
        for k in range(S):
            terms += [(d[k], r[k]), (d[k + 1], r[k])]
        return terms

    for k, total in enumerate(products(2 * S, keep, cross)):
        put(DR + k, total)
    sums[...] = jnp.sum(parts[...].T, axis=0, keepdims=True)


def coefficients(sums):
    tall = 24
    shape = (tall, 128)
    i = lax.broadcasted_iota(jnp.int32, shape, 0)
    j = lax.broadcasted_iota(jnp.int32, shape, 1)
    row_r, col_r = i > S, j > S
    a = jnp.where(row_r, i - (S + 1), i)
    b = jnp.where(col_r, j - (S + 1), j)
    valid = jnp.logical_and(i < COLS, j < COLS)
    base = jnp.where(row_r, jnp.where(col_r, RR, DR), jnp.where(col_r, DR, DD))
    at_plus = jnp.where(valid, base + a + b, -1)
    at_minus = jnp.where(valid, base + jnp.abs(a - b), -1)
    at_base = jnp.where(valid, base + ((a + b) & 1), -1)
    gram = jnp.zeros(shape, jnp.float32)
    for place in range(SUMS):
        weight = (
            (at_plus == place).astype(jnp.float32)
            + (at_minus == place).astype(jnp.float32)
            - (at_base == place).astype(jnp.float32)
        )
        gram = gram + weight * sums[:, place : place + 1]

    def change(index, axis):
        second = index > S
        k = jnp.where(second, index - (S + 1), index)
        count = jnp.where(second, S, S + 1)
        valid = index < COLS
        middle = jnp.where(jnp.logical_and(valid, k < count - 1), 6.0, 0.0)
        below = jnp.where(jnp.logical_and(valid, k >= 1), jnp.where(k == 1, 6.0, 3.0), 0.0)
        above = jnp.where(jnp.logical_and(valid, k + 1 < count - 1), 3.0, 0.0)
        size = shape[axis]

        def apply(v):
            return middle * v + below * pltpu.roll(v, 1, axis) + above * pltpu.roll(v, size - 1, axis)

        return apply

    down, along = change(i, 0), change(j, 1)

    def quadratic(left_down, right_along):
        return jnp.sum(left_down * (gram * right_along), keepdims=True)

    def unit(index, k):
        return (index == k).astype(jnp.float32)

    q_d, q_a = unit(i, 0), unit(j, 0)
    w_d, w_a = unit(i, S + 1), unit(j, S + 1)
    c_d = jnp.zeros(shape, jnp.float32)
    rho = quadratic(w_d, w_a)
    for _ in range(S):
        m_d, m_a = down(q_d), along(q_a)
        alpha = rho / quadratic(q_d, m_a)
        c_d = c_d + alpha * q_d
        w_d, w_a = w_d - alpha * m_d, w_a - alpha * m_a
        rho_new = quadratic(w_d, w_a)
        beta = rho_new / rho
        q_d, q_a = w_d + beta * q_d, w_a + beta * q_a
        rho = rho_new
    return c_d, w_d, q_d


def combine_kernel(sums, *refs):
    chain_d, chain_r, out, coefs = refs[: S + 1], refs[S + 1 : COLS], refs[COLS], refs[COLS + 1]
    total = jnp.sum(sums[...], axis=0, keepdims=True)
    for which, value in enumerate(coefficients(total)):
        coefs[which] = value
    keep = out.shape[4]
    tile = 16

    def body(step, _):
        plane, at = step // (keep // tile), step % (keep // tile)
        row = pl.multiple_of(at * tile, tile)
        source = pl.ds(pl.multiple_of(PAD + HALO + row, 8), tile)
        sums = [[None] * 3, [None] * 3]
        for k in range(COLS):
            chain, power, steps = (chain_d, k, S) if k <= S else (chain_r, k - S - 1, S - 1)
            low = chain_plan(steps)[0][power]
            factors = [coefs[which, k : k + 1, :] for which in range(3)]
            for h in range(2):
                v = chain[power][HALO + plane - low, h, source]
                for which in range(3):
                    term = v * factors[which]
                    sums[h][which] = term if k == 0 else sums[h][which] + term
        for h in range(2):
            for which in range(3):
                out[plane // 2, which, plane % 2, h, pl.ds(row, tile)] = sums[h][which]
        return 0

    lax.fori_loop(0, PLANES * (keep // tile), body, 0)


def finish_kernel(solution, back, out_x, out_r, out_d, hold, sem):
    pieces, _, per, halves, keep, _ = back.shape
    copies = []
    for which, out in ((1, out_r), (2, out_d), (0, out_x)):
        for g in range(pieces):
            for h in range(halves):
                for plane in range(per):
                    value = back[g, which, plane, h]
                    where = (plane, pl.ds(g * keep, keep), pl.ds(h * HALF, HALF))
                    if which == 0:
                        value = value + solution[where]
                    hold[(which, *where)] = value
        copies.append(pltpu.make_async_copy(hold.at[which], out, sem.at[which]))
        copies[-1].start()
    for copy in copies:
        copy.wait()


def on_device(solution, residual, direction):
    groups = lax.axis_size("x")
    x, c, zz = lax.axis_index("x"), lax.axis_index("c"), lax.axis_index("zz")
    outer = lax.axis_size("zz")
    per, height, lanes = direction.shape
    keep = height // groups
    rows = keep + 2 * HALO
    f32 = jnp.float32

    piece = jax.ShapeDtypeStruct((groups, per, 2, rows, HALF), f32)
    pieces = pl.pallas_call(
        pack_kernel,
        out_shape=(piece, piece),
        in_specs=[HBM, HBM],
        out_specs=(VMEM, VMEM),
        scratch_shapes=[pltpu.SemaphoreType.DMA((4 * groups,))],
        compiler_params=pltpu.CompilerParams(vmem_limit_bytes=8 * 2**20),
        name="pack",
    )(direction, residual)

    blocks = 2 * outer
    near = [(b, b - 1) for b in range(0, blocks, 2) if b > 0] + [(b, b + 1) for b in range(1, blocks, 2) if b + 1 < blocks]
    place = jnp.stack(
        [
            c,
            1 - jnp.logical_and(zz == 0, c == 0).astype(jnp.int32),
            1 - jnp.logical_and(zz == outer - 1, c == 1).astype(jnp.int32),
            (x != 0).astype(jnp.int32),
            (x != groups - 1).astype(jnp.int32),
        ]
    ).astype(jnp.int32)

    def spread(piece):
        own = lax.all_to_all(piece, "x", 0, 0, tiled=True)
        across = lax.ppermute(own, ("zz", "c"), near)
        side = lax.ppermute(own, "c", [(0, 1), (1, 0)])
        return own, side, across

    def chain_shapes(steps):
        return [jax.ShapeDtypeStruct((held, 2, rows + 2 * PAD, HALF), f32) for held in chain_plan(steps)[2]]

    around_d = spread(pieces[0])
    around_r = spread(pieces[1])
    sideways = pltpu.VMEM((GROUP, 2, rows, HALF), f32)
    shapes_d, shapes_r = chain_shapes(S), chain_shapes(S - 1)
    *chain_d, parts = pl.pallas_call(
        direction_kernel,
        out_shape=(*shapes_d, jax.ShapeDtypeStruct((128, 128), f32)),
        in_specs=[SMEM] + [VMEM] * 3,
        out_specs=(VMEM,) * (S + 2),
        scratch_shapes=[sideways],
        compiler_params=pltpu.CompilerParams(vmem_limit_bytes=4 * 2**20),
        cost_estimate=pl.CostEstimate(flops=10**8, bytes_accessed=10**6, transcendentals=0),
        name="direction_chain",
    )(place, *around_d)
    *chain_r, sums = pl.pallas_call(
        residual_kernel,
        out_shape=(*shapes_r, jax.ShapeDtypeStruct((1, 128), f32)),
        in_specs=[SMEM] + [VMEM] * (3 + S + 2),
        out_specs=(VMEM,) * (S + 1),
        scratch_shapes=[sideways, pltpu.VMEM((128, 128), f32)],
        compiler_params=pltpu.CompilerParams(vmem_limit_bytes=4 * 2**20),
        cost_estimate=pl.CostEstimate(flops=10**8, bytes_accessed=10**6, transcendentals=0),
        name="residual_chain",
    )(place, *around_r, *chain_d, parts)

    devices = groups * blocks
    everyone = lax.all_to_all(jnp.broadcast_to(sums[None], (devices, 1, 128)), ALL, 0, 0, tiled=True)

    mixed = pl.pallas_call(
        combine_kernel,
        out_shape=jax.ShapeDtypeStruct((groups, 3, per, 2, keep, HALF), f32),
        in_specs=[VMEM] * (COLS + 1),
        out_specs=VMEM,
        scratch_shapes=[pltpu.VMEM((3, 24, 128), f32)],
        compiler_params=pltpu.CompilerParams(vmem_limit_bytes=4 * 2**20),
        name="combine",
    )(everyone.reshape(devices, 128), *chain_d, *chain_r)

    back = lax.all_to_all(mixed, "x", 0, 0, tiled=True)
    whole = jax.ShapeDtypeStruct((per, height, lanes), f32)
    return pl.pallas_call(
        finish_kernel,
        out_shape=(whole,) * 3,
        in_specs=[VMEM, VMEM],
        out_specs=(HBM,) * 3,
        scratch_shapes=[pltpu.VMEM((3, per, height, lanes), f32), pltpu.SemaphoreType.DMA((3,))],
        compiler_params=pltpu.CompilerParams(vmem_limit_bytes=8 * 2**20),
        name="finish",
    )(solution, back)


def solution(mesh):
    blocks, groups = mesh.devices.shape
    split = Mesh(mesh.devices.reshape(blocks // 2, 2, groups), ALL)
    spec = P(ALL, None, None)
    return jax.shard_map(
        on_device, mesh=split, in_specs=(spec, spec, spec), out_specs=(spec, spec, spec), check_vma=False
    )
```

time: 131 us -> 115 us (0.88)
  waiting for transfers between devices: 15.1 us -> 3.46 us
  starting transfers between devices: 5.37 us -> 15.4 us
  blocking collectives: 70.2 us -> 63.7 us
  Pallas kernels: 34.4 us -> 29.6 us
  other arithmetic: 2.46 us -> 0 us
    ppermute x2 -> x4, waiting for transfers between devices: 15.1 us -> 0.01 us  [the longest x2 0.01 us: spread(): across = lax.ppermute(own, ('zz', 'c'), near)]
    all_to_all x1, blocking collectives: 21.6 us -> 14.6 us  [spread(): own = lax.all_to_all(piece, 'x', 0, 0, tiled=True)]
    ppermute x2 -> x4, starting transfers between devices: 5.37 us -> 11.9 us  [the longest x2 11.7 us: spread(): across = lax.ppermute(own, ('zz', 'c'), near)]
    pallas_call x1 -> x4, Pallas kernels: 29.2 us -> 24.3 us  [the longest x1 11.1 us: on_device(): pl.pallas_call(direction_kernel, out_shape=(*shapes_d, jax.ShapeDtypeStru...]
    all_to_all x0 -> x1, starting transfers between devices: none -> 3.48 us  [spread(): own = lax.all_to_all(piece, 'x', 0, 0, tiled=True)]
    all_to_all x0 -> x1, waiting for transfers between devices: none -> 3.45 us  [spread(): own = lax.all_to_all(piece, 'x', 0, 0, tiled=True)]
    transpose x4 -> x0, local copies, waits for them, and re-layouts: 1.87 us -> none  [on_device(): jnp.swapaxes(back[:, which], 0, 1).reshape(per, height, lanes)]
    unnamed x6, local copies, waits for them, and re-layouts: 0.47 us -> 2.08 us
  transfers between devices with their start and end apart: 2 -> 5, of which waited for: 1 -> 1; matrix products, arithmetic and copies ran while one was open for 0% -> 0% of each run, Pallas kernels for 0% -> 10%
where the time goes in v1:
time: 115 us
  blocking collectives  63.7 us (55%)
  Pallas kernels  29.6 us (26%)
  starting transfers between devices  15.4 us (13%)
  waiting for transfers between devices  3.46 us (3%)
  local copies, waits for them, and re-layouts  2.24 us (2%)
    all_to_all x1, blocking collectives, on_device(): lax.all_to_all(jnp.broadcast_to(sums[None], (devices, 1, 128)), ALL, 0, 0...  26.6 us
    all_to_all x1, blocking collectives, on_device(): back = lax.all_to_all(mixed, 'x', 0, 0, tiled=True)  22.4 us
    all_to_all x1, blocking collectives, spread(): own = lax.all_to_all(piece, 'x', 0, 0, tiled=True)  14.6 us
    ppermute x2, starting transfers between devices, spread(): across = lax.ppermute(own, ('zz', 'c'), near)  11.7 us
    pallas_call x1, Pallas kernels, on_device(): pl.pallas_call(direction_kernel, out_shape=(*shapes_d, jax.ShapeDtypeStru...  11.1 us
    pallas_call x1, Pallas kernels, on_device(): pl.pallas_call(residual_kernel, out_shape=(*shapes_r, jax.ShapeDtypeStruc...  10.8 us
    pallas_call x1, Pallas kernels, on_device(): pl.pallas_call(combine_kernel, out_shape=jax.ShapeDtypeStruct((groups, 3,...  5.26 us
    all_to_all x1, starting transfers between devices, spread(): own = lax.all_to_all(piece, 'x', 0, 0, tiled=True)  3.48 us
  transfers between devices with their start and end apart: 5, of which 1 were waited for; matrix products, arithmetic and copies ran while one was open for 0% of the time, Pallas kernels for 10%

profile of v1, /device:TPU:1, one launch (start us, length us, event | category | flops | bytes accessed | tf_op | source)
XLA Modules:
  0.0 115.1 jit_solution(10699325558591566855)
XLA Ops:
  0.6 0.0 copy-start
  0.6 1.0 copy-done
  1.7 0.0 copy-start.1
  1.7 1.0 copy-done.1
  2.7 1.1 pack.1
  3.9 14.6 %all_to_all.20.own = f32[4,2,2,80,128]{4,3,2,1,0:T(8,128)S(1)} all-to-all(f32[4,2,2,80,128]{4,3,2,1,0:T(8,128)S(1)} %get-tuple-element.25), channel_id=1, replica_groups=mesh['zz'=32,'c'=2,'x'=4] {'x'}, dimensions={0} | all-to-all | bytes 1310720 | tf_op jit(solution)/shard_map/all_to_all | solution.py:369
  18.5 3.5 %all-to-all-start = ((f32[4,2,2,80,128]{4,3,2,1,0:T(8,128)}), f32[4,2,2,80,128]{4,3,2,1,0:T(8,128)S(1)}, u32[]{:S(2)}, u32[]{:S(2)}) async-start(f32[4,2,2,80,128]{4,3,2,1,0:T(8,128)} %get-tuple-element.24), calls=%async_computation | async-start | bytes 1310720 | tf_op jit(solution)/shard_map/all_to_all | solution.py:369
  22.0 5.3 %collective-permute-start.3 = (f32[4,2,2,80,128]{4,3,2,1,0:T(8,128)S(1)}, f32[4,2,2,80,128]{4,3,2,1,0:T(8,128)S(1)}, u32[]{:S(2)}, u32[]{:S(2)}) collective-permute-start(f32[4,2,2,80,128]{4,3,2,1,0:T(8,128)S(1)} %all_to_all.20.own), channel_id=1, source_target_pairs={{8,4},{16,12},{24,20},{32,28},{40,36},{48,44},{56,52},{64,60},{72,... | collective-permute-start | bytes 1966088 | tf_op jit(solution)/shard_map/ppermute | solution.py:370
  27.3 0.1 collective-permute-start.2
  27.4 3.4 %all-to-all-done.own = f32[4,2,2,80,128]{4,3,2,1,0:T(8,128)S(1)} async-done(((f32[4,2,2,80,128]{4,3,2,1,0:T(8,128)}), f32[4,2,2,80,128]{4,3,2,1,0:T(8,128)S(1)}, u32[]{:S(2)}, u32[]{:S(2)}) %all-to-all-start) | async-done | bytes 655392 | tf_op jit(solution)/shard_map/all_to_all | solution.py:369
  30.8 6.4 %collective-permute-start.1 = (f32[4,2,2,80,128]{4,3,2,1,0:T(8,128)S(1)}, f32[4,2,2,80,128]{4,3,2,1,0:T(8,128)S(1)}, u32[]{:S(2)}, u32[]{:S(2)}) collective-permute-start(f32[4,2,2,80,128]{4,3,2,1,0:T(8,128)S(1)} %all-to-all-done.own), channel_id=1, source_target_pairs={{8,4},{16,12},{24,20},{32,28},{40,36},{48,44},{56,52},{64,60},{72,... | collective-permute-start | bytes 1966088 | tf_op jit(solution)/shard_map/ppermute | solution.py:370
  37.2 0.1 collective-permute-start
  37.4 0.1 stack.31.place
  37.4 0.0 collective-permute-done.3.across
  37.4 0.0 collective-permute-done.2.side
  37.4 11.1 %direction_chain.1 = (f32[26,2,96,128]{3,2,1,0:T(8,128)S(1)}, f32[24,2,96,128]{3,2,1,0:T(8,128)S(1)}, f32[22,2,96,128]{3,2,1,0:T(8,128)S(1)}, f32[20,2,96,128]{3...) custom-call(s32[5]{0:T(128)S(1)} %stack.31.place, ...), custom_call_target="tpu_custom_call" | custom-call | flops 100000000 | bytes 1000000 | tf_op jit(solution)/shard_map/direction_chain/pallas_call | solution.py:381
  48.6 0.0 collective-permute-done.1.across
  48.6 0.0 collective-permute-done.side
  48.6 10.8 %residual_chain.1 = (f32[22,2,96,128]{3,2,1,0:T(8,128)S(1)}, f32[22,2,96,128]{3,2,1,0:T(8,128)S(1)}, f32[20,2,96,128]{3,2,1,0:T(8,128)S(1)}, f32[18,2,96,128]{3,...) custom-call(s32[5]{0:T(128)S(1)} %stack.31.place, ...), custom_call_target="tpu_custom_call" | custom-call | flops 100000000 | bytes 1000000 | tf_op jit(solution)/shard_map/residual_chain/pallas_call | solution.py:391
  59.5 0.1 broadcast_in_dim.9
  59.5 26.6 %all_to_all.21 = f32[256,1,128]{2,1,0:T(1,128)S(1)} all-to-all(f32[256,1,128]{2,1,0:T(1,128)S(1)} %broadcast_in_dim.9), channel_id=1, replica_groups=mesh['zz'=32,'c'=2,'x'=4] {'zz','c','x'}, dimensions={0} | all-to-all | bytes 262144 | tf_op jit(solution)/shard_map/all_to_all | solution.py:403
  86.2 5.3 %combine.1 = f32[4,3,2,2,64,128]{5,4,3,2,1,0:T(8,128)S(1)} custom-call(f32[256,128]{1,0:T(8,128)S(1)} %bitcast.7, f32[26,2,96,128]{3,2,1,0:T(8,128)S(1)} %get-tuple-element.26.refs_0_, f32[24,2,96,128]{3,2,1,0:T(8,128)S(1)} %get-tuple-element.27.refs_1_, f32[22,2,96,128]{3,2,1,0:T(8,128)S(1)} %get-tuple-element.28.refs_2_, ...), custom_call_target="tpu_custom_call" | custom-call | tf_op jit(solution)/shard_map/combine/pallas_call | solution.py:405
  91.4 0.0 copy-start.2
  91.5 22.4 %all_to_all.22.back = f32[4,3,2,2,64,128]{5,4,3,2,1,0:T(8,128)S(1)} all-to-all(f32[4,3,2,2,64,128]{5,4,3,2,1,0:T(8,128)S(1)} %combine.1), channel_id=1, replica_groups=mesh['zz'=32,'c'=2,'x'=4] {'x'}, dimensions={0} | all-to-all | bytes 3145728 | tf_op jit(solution)/shard_map/all_to_all | solution.py:415
  113.9 0.0 copy-done.2
  113.9 1.2 %finish.1 = (f32[2,256,256]{2,1,0:T(8,128)}, f32[2,256,256]{2,1,0:T(8,128)}, f32[2,256,256]{2,1,0:T(8,128)}) custom-call(f32[2,256,256]{2,1,0:T(8,128)S(1)} %copy-done.2, f32[4,3,2,2,64,128]{5,4,3,2,1,0:T(8,128)S(1)} %all_to_all.22.back), custom_call_target="tpu_custom_call" | custom-call | tf_op jit(solution)/shard_map/finish/pallas_call | solution.py:417
Async XLA Ops:
  0.6 1.0 copy-start
  1.7 1.0 copy-start.1
  18.5 12.3 %all-to-all-start = ((f32[4,2,2,80,128]{4,3,2,1,0:T(8,128)}), f32[4,2,2,80,128]{4,3,2,1,0:T(8,128)S(1)}, u32[]{:S(2)}, u32[]{:S(2)}) async-start(f32[4,2,2,80,128]{4,3,2,1,0:T(8,128)} %get-tuple-element.24), calls=%async_computation | async-start | bytes 1310720 | tf_op jit(solution)/shard_map/all_to_all | solution.py:369
  22.0 15.5 %collective-permute-start.3 = (f32[4,2,2,80,128]{4,3,2,1,0:T(8,128)S(1)}, f32[4,2,2,80,128]{4,3,2,1,0:T(8,128)S(1)}, u32[]{:S(2)}, u32[]{:S(2)}) collective-permute-start(f32[4,2,2,80,128]{4,3,2,1,0:T(8,128)S(1)} %all_to_all.20.own), channel_id=1, source_target_pairs={{8,4},{16,12},{24,20},{32,28},{40,36},{48,44},{56,52},{64,60},{72,... | collective-permute-start | bytes 1966088 | tf_op jit(solution)/shard_map/ppermute | solution.py:370
  27.3 10.2 %collective-permute-start.2 = (f32[4,2,2,80,128]{4,3,2,1,0:T(8,128)S(1)}, f32[4,2,2,80,128]{4,3,2,1,0:T(8,128)}, u32[]{:S(2)}, u32[]{:S(2)}) collective-permute-start(f32[4,2,2,80,128]{4,3,2,1,0:T(8,128)S(1)} %all_to_all.20.own), channel_id=1, source_target_pairs={{0,4},{4,0},{1,5},{5,1},{2,6},{6,2},{3,7},{7,3},{8,12},{12,8},{9,1... | collective-permute-start | bytes 1966088 | tf_op jit(solution)/shard_map/ppermute | solution.py:371
  30.8 17.8 %collective-permute-start.1 = (f32[4,2,2,80,128]{4,3,2,1,0:T(8,128)S(1)}, f32[4,2,2,80,128]{4,3,2,1,0:T(8,128)S(1)}, u32[]{:S(2)}, u32[]{:S(2)}) collective-permute-start(f32[4,2,2,80,128]{4,3,2,1,0:T(8,128)S(1)} %all-to-all-done.own), channel_id=1, source_target_pairs={{8,4},{16,12},{24,20},{32,28},{40,36},{48,44},{56,52},{64,60},{72,... | collective-permute-start | bytes 1966088 | tf_op jit(solution)/shard_map/ppermute | solution.py:370
  37.2 11.4 %collective-permute-start = (f32[4,2,2,80,128]{4,3,2,1,0:T(8,128)S(1)}, f32[4,2,2,80,128]{4,3,2,1,0:T(8,128)S(1)}, u32[]{:S(2)}, u32[]{:S(2)}) collective-permute-start(f32[4,2,2,80,128]{4,3,2,1,0:T(8,128)S(1)} %all-to-all-done.own), channel_id=1, source_target_pairs={{0,4},{4,0},{1,5},{5,1},{2,6},{6,2},{3,7},{7,3},{8,12},{12,8},{9,1... | collective-permute-start | bytes 1966088 | tf_op jit(solution)/shard_map/ppermute | solution.py:371
  91.4 22.4 %copy-start.2 = (f32[2,256,256]{2,1,0:T(8,128)S(1)}, f32[2,256,256]{2,1,0:T(8,128)}, u32[]{:S(2)}) copy-start(f32[2,256,256]{2,1,0:T(8,128)} %solution.1) | copy-start | bytes 1572868
